TPU v7x, 256 devices: a whole 4x4x8 slice. The times are simulated.
256 devices in a mesh: ens: 4 (over x), slab: 64 (over y, z, core).
Axes of the slice: x: 4, y: 4, z: 8, core: 2. Of those that a mesh axis runs over, the one named last changes fastest.
Arguments:
- velocity: float32 [4, 3, 8, 2048, 1024], P('ens', None, None, 'slab'), may hold values from -6 to 6
- cutoffs: int32 [4, 2, 8], P('ens'), may hold values from 128 to 511, as said below
- plane_index: int32 [4], P('ens'), may hold values from 0 to 2047
- boundary_index: int32 [4], P('ens'), may hold values from 0 to 2047
Outputs:
- blended: float32 [4, 3, 8, 2048, 1024], P('ens', None, None, 'slab')
Inputs may be any that keep to these rules, and one draw needn't show every extreme that they name: `cutoffs`: row 0 lies in 256 to 511 and row 1 in 128 to 255; in every member some level has row 0 equal to 511 and some level has row 1 equal to 255.
All inputs are finite; a program needn't handle non-finite values.
Results may differ from a plain program's by a relative error of at most 0.0003.
Values sent between devices are 32-bit elements; how exact they have to be, the bound alone decides.
A program may use at most 128 MiB of HBM per device.

v0:
```python
import functools

import jax
import jax.numpy as jnp
import ml_dtypes
import numpy as np
from jax import lax
from jax.experimental import pallas as pl
from jax.experimental.pallas import tpu as pltpu
from jax.sharding import PartitionSpec as P

MESH = pl.DeviceIdType.MESH
KX = 512
KY = 256
SLABS = 64
F32 = jnp.float32
BF16 = jnp.bfloat16


def split_table(table):
    high = table.astype(ml_dtypes.bfloat16)
    low = (table - high.astype(np.float64)).astype(ml_dtypes.bfloat16)
    return np.stack([high, low])


def half_basis(length, modes):
    position = np.arange(length // 2)
    tables = []
    for parity in (0, 1):
        wavenum = np.arange(parity, modes, 2)
        angles = (position[:, None] * wavenum[None, :] % length) * (2.0 * np.pi / length)
        tables.append(split_table(np.concatenate([np.cos(angles), np.sin(angles)], axis=1)))
    return np.stack(tables)


def dot(a, b):
    return lax.dot_general(a, b, (((1,), (0,)), ((), ())), preferred_element_type=F32)


def dot_nt(a, b):
    return lax.dot_general(a, b, (((1,), (1,)), ((), ())), preferred_element_type=F32)


def split(value):
    high = value.astype(BF16)
    return high, (value - high.astype(F32)).astype(BF16)


def exchange_groups(parts):
    lane = lax.broadcasted_iota(jnp.int32, parts[0].shape, parts[0].ndim - 1)
    axis = parts[0].ndim - 1
    for bit, width in ((1, 32), (2, 64)):
        first = (lane // width) % 2 == 0
        done = list(parts)
        for a in range(4):
            if a & bit:
                continue
            u, v = parts[a], parts[a | bit]
            done[a] = jnp.where(first, u, pltpu.roll(v, width, axis))
            done[a | bit] = jnp.where(first, pltpu.roll(u, 128 - width, axis), v)
        parts = done
    return parts


def filter_kernel(
    vel, cut, plane, bound, ytab, xtab, xtab_t,
    ret,
    u, yt, xt, xtt, spec, recv, data, mask, coef, parts, field, back, relax, plane_out, plane_in,
    load, table, send_f, recv_f, send_r, recv_r, send_p, recv_p,
):
    ens = lax.axis_index("ens")
    me = lax.axis_index("slab")
    my_y, my_z, my_c = lax.div(me, 16), lax.rem(lax.div(me, 2), 8), lax.rem(me, 2)
    after, before = lax.rem(ens + 1, 4), lax.rem(ens + 3, 4)

    def other(i):
        y = lax.rem(my_y + lax.rem(lax.div(i, 2), 4), 4)
        z = lax.rem(my_z + lax.div(i, 8), 8)
        c = lax.rem(my_c + lax.rem(i, 2), 2)
        return y * 16 + z * 2 + c

    loads = [pltpu.make_async_copy(vel.at[c], u.at[c], load.at[c]) for c in range(3)]
    tables = [pltpu.make_async_copy(a, b, table.at[i]) for i, (a, b) in enumerate(((ytab, yt), (xtab, xt), (xtab_t, xtt)))]
    loads[0].start()
    tables[0].start()

    barrier = pltpu.get_barrier_semaphore()

    def greet(i, _):
        pl.semaphore_signal(barrier, 1, device_id={"ens": ens, "slab": other(i)}, device_id_type=MESH)
        return 0

    lax.fori_loop(1, SLABS, greet, 0)
    for e in (after, before):
        pl.semaphore_signal(barrier, 1, device_id={"ens": e, "slab": me}, device_id_type=MESH)
    for copy in (loads[1], loads[2], tables[1], tables[2]):
        copy.start()

    def spread(source, target, c, sent, landed):
        def one(i, _):
            t = other(i)
            pltpu.make_async_remote_copy(
                source.at[c, t], target.at[c, me], sent.at[c], landed.at[c],
                device_id={"ens": ens, "slab": t}, device_id_type=MESH,
            ).start()
            return 0

        lax.fori_loop(1, SLABS, one, 0)

    def all_of(buffer, c, sem):
        blocks = buffer.at[c, pl.ds(0, SLABS - 1)]
        pltpu.make_async_copy(blocks, blocks, sem.at[c]).wait()

    def analyse(c):
        pltpu.make_async_copy(vel.at[c], u.at[c], load.at[c]).wait()
        left, right = u[c, :, :512], u[c, :, 512:]
        for parity in (0, 1):
            high, low = split(left + right if parity == 0 else left - right)
            total = dot_nt(yt[parity, 0], high) + (dot_nt(yt[parity, 0], low) + dot_nt(yt[parity, 1], high))
            spec[c, pl.ds(32 * parity, 32)] = total.reshape(32, 8, 256)

    tables[0].wait()
    analyse(0)
    pl.semaphore_wait(barrier, SLABS + 1)

    def forward(c, _):
        @pl.when(c > 0)
        def _():
            analyse(c)

        spread(spec, recv, c, send_f, recv_f)
        recv[c, me] = spec[c, me]
        return 0

    lax.fori_loop(0, 3, forward, 0)

    row = lax.broadcasted_iota(jnp.int32, (8, 512), 0)
    column = lax.broadcasted_iota(jnp.int32, (8, 512), 1)
    ky = 2 * ((8 * me + row) % 128) + lax.div(me, 32)
    weight_y = jnp.where(ky == 0, 1.0, 2.0) / 1024.0
    for parity in (0, 1):
        kx = 2 * (column % 256) + parity
        weight = weight_y * (jnp.where(kx == 0, 1.0, 2.0) / 2048.0)
        for z in range(8):
            kept = jnp.logical_and(kx <= cut[0, z], ky <= cut[1, z])
            mask[parity, pl.ds(8 * z, 8), :] = jnp.where(kept, weight, 0.0)
    lane = lax.broadcasted_iota(jnp.int32, (8, 128), 1)
    for q in range(16):
        offset = jnp.abs(128 * q + lane - bound[0])
        distance = jnp.minimum(offset, 2048 - offset)
        relax[q] = jnp.exp(-distance.astype(F32) / 512.0)
    tables[1].wait()
    tables[2].wait()

    def filter_chunk(c, _):
        all_of(recv, c, recv_f)

        def gather(q, _):
            at = pl.ds(pl.multiple_of(128 * q, 128), 128)
            for h in (0, 1):
                pieces = [(recv[c, 4 * q + a, :, pl.ds(128 * h, 128)], recv[c, 32 + 4 * q + a, :, pl.ds(128 * h, 128)]) for a in range(4)]
                for parity in (0, 1):
                    mixed = exchange_groups([m + n if parity == 0 else m - n for m, n in pieces])
                    high, low = split(jnp.concatenate(mixed, axis=0))
                    data[parity, pl.ds(32 * h, 32), at] = high
                    data[parity, pl.ds(64 + 32 * h, 32), at] = low
            return 0

        lax.fori_loop(0, 8, gather, 0)
        for parity in (0, 1):
            both = dot(data[parity], xt[parity, 0])
            kept = (both[:64] + (both[64:] + dot(data[parity, :64], xt[parity, 1]))) * mask[parity]
            high, low = split(kept)
            coef[:64] = high
            coef[64:] = low
            both = dot(coef[...], xtt[parity, 0])
            parts[parity] = both[:64] + (both[64:] + dot(coef[:64], xtt[parity, 1]))

        xi = lax.broadcasted_iota(jnp.int32, (64, 128), 1)

        def combine(q, picked):
            at = pl.ds(pl.multiple_of(128 * q, 128), 128)
            even, odd = parts[0, :, at], parts[1, :, at]
            near, far = even + odd, even - odd
            field[0, :, at] = near
            field[1, :, at] = far
            x = xi + 128 * q
            return picked + (jnp.where(x == plane[0], near, 0.0) + jnp.where(x + 1024 == plane[0], far, 0.0))

        picked = lax.fori_loop(0, 8, combine, jnp.zeros((64, 128), F32))
        plane_out[c] = jnp.broadcast_to(jnp.sum(picked, axis=1, keepdims=True), (64, 128))
        handed = pltpu.make_async_remote_copy(
            plane_out.at[c], plane_in.at[c], send_p.at[c], recv_p.at[c],
            device_id={"ens": after, "slab": me}, device_id_type=MESH,
        )
        handed.start()
        handed.wait_recv()

        def scatter(q, _):
            at = pl.ds(pl.multiple_of(128 * q, 128), 128)
            for half in (0, 1):
                weight = relax[8 * half + q]
                for h in (0, 1):
                    rows = []
                    for b in range(4):
                        own = field[half, pl.ds(32 * h + 8 * b, 8), at]
                        rows.append(own + weight * (plane_in[c, pl.ds(32 * h + 8 * b, 8), :] - own))
                    for a, piece in enumerate(exchange_groups(rows)):
                        back[c, 32 * half + 4 * q + a, :, pl.ds(128 * h, 128)] = piece
            return 0

        lax.fori_loop(0, 8, scatter, 0)
        spread(back, ret, c, send_r, recv_r)
        ret[c, me] = back[c, me]
        return 0

    lax.fori_loop(0, 3, filter_chunk, 0)

    def finish(c, _):
        all_of(recv, c, send_f)
        all_of(recv, c, send_r)
        all_of(recv, c, recv_r)
        pltpu.make_async_copy(plane_out.at[c], plane_out.at[c], send_p.at[c]).wait()
        return 0

    lax.fori_loop(0, 3, finish, 0)


def synthesis_kernel(ret, yt, out):
    halves = []
    for parity in (0, 1):
        high, low = split(ret[0, pl.ds(256 * parity, 256), :].T)
        halves.append(dot(high, yt[parity, 0]) + (dot(low, yt[parity, 0]) + dot(high, yt[parity, 1])))
    out[0, :, :512] = halves[0] + halves[1]
    out[0, :, 512:] = halves[0] - halves[1]


def on_device(velocity, cutoffs, plane_index, boundary_index):
    ytab = jnp.asarray(np.ascontiguousarray(half_basis(1024, KY).transpose(0, 1, 3, 2)))
    x_basis = half_basis(2048, KX)
    xtab = jnp.asarray(x_basis)
    xtab_t = jnp.asarray(np.ascontiguousarray(x_basis.transpose(0, 1, 3, 2)))
    anywhere = pl.BlockSpec(memory_space=pltpu.HBM)
    smem = pl.BlockSpec(memory_space=pltpu.SMEM)
    dma = pltpu.SemaphoreType.DMA
    blocks = pltpu.VMEM((3, SLABS, 8, 256), F32)
    ret = pl.pallas_call(
        filter_kernel,
        out_shape=jax.ShapeDtypeStruct((3, SLABS, 8, 256), F32),
        in_specs=[anywhere, smem, smem, smem, anywhere, anywhere, anywhere],
        out_specs=pl.BlockSpec(memory_space=pltpu.VMEM),
        scratch_shapes=[
            pltpu.VMEM((3, 256, 1024), F32),
            pltpu.VMEM(ytab.shape, BF16),
            pltpu.VMEM(xtab.shape, BF16),
            pltpu.VMEM(xtab_t.shape, BF16),
            blocks,
            blocks,
            pltpu.VMEM((2, 128, 1024), BF16),
            pltpu.VMEM((2, 64, 512), F32),
            pltpu.VMEM((128, 512), BF16),
            pltpu.VMEM((2, 64, 1024), F32),
            pltpu.VMEM((2, 64, 1024), F32),
            blocks,
            pltpu.VMEM((16, 8, 128), F32),
            pltpu.VMEM((3, 64, 128), F32),
            pltpu.VMEM((3, 64, 128), F32),
        ]
        + [dma((3,))] * 8,
        compiler_params=pltpu.CompilerParams(collective_id=0, has_side_effects=True, vmem_limit_bytes=48 << 20),
    )(velocity.reshape(3, 256, 1024), cutoffs[0], plane_index, boundary_index, ytab, xtab, xtab_t)
    out = pl.pallas_call(
        synthesis_kernel,
        grid=(3,),
        out_shape=jax.ShapeDtypeStruct((3, 256, 1024), F32),
        in_specs=[
            pl.BlockSpec((1, 512, 256), lambda i: (i, 0, 0)),
            pl.BlockSpec(ytab.shape, lambda i: (0, 0, 0, 0)),
        ],
        out_specs=pl.BlockSpec((1, 256, 1024), lambda i: (i, 0, 0)),
    )(ret.reshape(3, 512, 256), ytab)
    return out.reshape(velocity.shape)


def solution(mesh):
    in_specs = (P("ens", None, None, "slab", None), P("ens", None, None), P("ens"), P("ens"))
    out_specs = P("ens", None, None, "slab", None)
    return jax.shard_map(on_device, mesh=mesh, in_specs=in_specs, out_specs=out_specs, check_vma=False)
```

profile of v0, /device:TPU:1, one launch (start us, length us, event | category | flops | bytes accessed | tf_op | source)
XLA Modules:
  0.0 94.3 jit_solution(434290513706700065)
XLA Ops:
  1.3 0.0 copy-start.1
  1.3 1.2 %copy-done.1 = bf16[2,2,256,512]{3,2,1,0:T(8,128)(2,1)S(1)} copy-done((bf16[2,2,256,512]{3,2,1,0:T(8,128)(2,1)S(1)}, bf16[2,2,256,512]{3,2,1,0:T(8,128)(2,1)}, u32[]{:S(2)}) %copy-start.1) | copy-done | bytes 1048600
  2.5 0.0 copy-start.2
  2.5 1.9 %copy-done.2 = f32[1,3,8,32,1024]{4,3,2,1,0:T(8,128)S(1)} copy-done((f32[1,3,8,32,1024]{4,3,2,1,0:T(8,128)S(1)}, f32[1,3,8,32,1024]{4,3,2,1,0:T(8,128)}, u32[]{:S(2)}) %copy-start.2) | copy-done | bytes 3145752
  4.4 0.0 copy-start.3
  4.4 0.7 copy-done.3
  5.1 83.0 %shard_map.73 = f32[3,64,8,256]{3,2,1,0:T(8,128)S(1)} custom-call(f32[3,256,1024]{2,1,0:T(8,128)S(1)} %bitcast.5, s32[2,8]{1,0:T(2,128)S(1)} %bitcast.6, s32[1]{0:T(128)S(6)} %copy.8.plane, s32[1]{0:T(128)S(6)} %copy.9.bound, bf16[2,2,256,512]{3,2,1,0:T(8,128)(2,1)S(1)} %copy-done.1, bf16[2,2,1024,512]{3,2,1,0:T(8,128)(2,1)} %constant.7.clone.xtab, ...), custom_call_target="tpu_custom_call" | custom-call | tf_op jit(solution)/shard_map/pallas_call | solution.py:247
  88.1 0.0 copy-start
  88.1 1.2 %copy-done = f32[3,64,8,256]{3,2,1,0:T(8,128)} copy-done((f32[3,64,8,256]{3,2,1,0:T(8,128)}, f32[3,64,8,256]{3,2,1,0:T(8,128)S(1)}, u32[]{:S(2)}) %copy-start) | copy-done | bytes 1572888
  89.3 5.0 %shard_map.74 = f32[3,256,1024]{2,1,0:T(8,128)} custom-call(f32[3,512,256]{2,1,0:T(8,128)} %bitcast.4, bf16[2,2,256,512]{3,2,1,0:T(8,128)(2,1)} %constant.6.clone.ytab.yt), custom_call_target="tpu_custom_call" | custom-call | tf_op jit(solution)/shard_map/pallas_call | solution.py:272
Async XLA Ops:
  1.3 1.2 %copy-start.1 = (bf16[2,2,256,512]{3,2,1,0:T(8,128)(2,1)S(1)}, bf16[2,2,256,512]{3,2,1,0:T(8,128)(2,1)}, u32[]{:S(2)}) copy-start(bf16[2,2,256,512]{3,2,1,0:T(8,128)(2,1)} %constant.6.clone.ytab.yt) | copy-start | bytes 3145732
  2.5 1.9 %copy-start.2 = (f32[1,3,8,32,1024]{4,3,2,1,0:T(8,128)S(1)}, f32[1,3,8,32,1024]{4,3,2,1,0:T(8,128)}, u32[]{:S(2)}) copy-start(f32[1,3,8,32,1024]{4,3,2,1,0:T(8,128)} %param.7) | copy-start | bytes 9437188
  4.4 0.7 copy-start.3
  88.1 1.2 %copy-start = (f32[3,64,8,256]{3,2,1,0:T(8,128)}, f32[3,64,8,256]{3,2,1,0:T(8,128)S(1)}, u32[]{:S(2)}) copy-start(f32[3,64,8,256]{3,2,1,0:T(8,128)S(1)} %shard_map.73) | copy-start | bytes 4718596
where the time goes:
time: 94.6 us; the launch traced here: 94.3 us
  Pallas kernels  88.1 us (93%)
  local copies, waits for them, and re-layouts  4.95 us (5%)
  between operations  1.32 us (1%)
    pallas_call x1, Pallas kernels, on_device(): pl.pallas_call(filter_kernel, out_shape=jax.ShapeDtypeStruct((3, SLABS, 8...  83 us
    pallas_call x1, Pallas kernels, on_device(): pl.pallas_call(synthesis_kernel, grid=(3,), out_shape=jax.ShapeDtypeStruc...  5.04 us
    unnamed x8, local copies, waits for them, and re-layouts  4.95 us

commit v1 on v0

--- a/solution.py
+++ b/solution.py
@@ -13,6 +13,8 @@
 KX = 512
 KY = 256
 SLABS = 64
+VMEM_GRANT = 36 << 20
+AT_Y, AT_X, AT_XT = pl.ds(0, 2), pl.ds(2, 8), pl.ds(10, 8)
 F32 = jnp.float32
 BF16 = jnp.bfloat16
 
@@ -44,6 +46,16 @@
 def split(value):
     high = value.astype(BF16)
     return high, (value - high.astype(F32)).astype(BF16)
+
+
+def synthesise(coefficients, tab_y, out):
+    halves = []
+    for parity in (0, 1):
+        y_high, y_low = tab_y[parity, :256], tab_y[parity, 256:]
+        high, low = split(coefficients[256 * parity : 256 * parity + 256].T)
+        halves.append(dot(high, y_high) + (dot(low, y_high) + dot(high, y_low)))
+    out[:, :512] = halves[0] + halves[1]
+    out[:, 512:] = halves[0] - halves[1]
 
 
 def exchange_groups(parts):
@@ -63,10 +75,10 @@
 
 
 def filter_kernel(
-    vel, cut, plane, bound, ytab, xtab, xtab_t,
-    ret,
-    u, yt, xt, xtt, spec, recv, data, mask, coef, parts, field, back, relax, plane_out, plane_in,
-    load, table, send_f, recv_f, send_r, recv_r, send_p, recv_p,
+    vel, cut_at, plane, bound, tables,
+    first_out, second_out, last_out, tab_y,
+    cut, u, tab, spec, recv, data, mask, coef, parts, field, back, ret, ret_half, relax, plane_out, plane_in,
+    scalar, load, table, send_f, recv_f, send_r, recv_r, send_p, recv_p,
 ):
     ens = lax.axis_index("ens")
     me = lax.axis_index("slab")
@@ -74,15 +86,21 @@
     after, before = lax.rem(ens + 1, 4), lax.rem(ens + 3, 4)
 
     def other(i):
-        y = lax.rem(my_y + lax.rem(lax.div(i, 2), 4), 4)
-        z = lax.rem(my_z + lax.div(i, 8), 8)
-        c = lax.rem(my_c + lax.rem(i, 2), 2)
-        return y * 16 + z * 2 + c
+        i = i - 1
+        step = lax.div(i, 8)
+        dz = lax.rem(12 + (1 - 2 * lax.rem(step, 2)) * lax.div(step + 1, 2), 8)
+        dy, dc = 3 - lax.rem(lax.div(i, 2), 4), 1 - lax.rem(i, 2)
+        return lax.rem(my_y + dy, 4) * 16 + lax.rem(my_z + dz, 8) * 2 + lax.rem(my_c + dc, 2)
 
     loads = [pltpu.make_async_copy(vel.at[c], u.at[c], load.at[c]) for c in range(3)]
-    tables = [pltpu.make_async_copy(a, b, table.at[i]) for i, (a, b) in enumerate(((ytab, yt), (xtab, xt), (xtab_t, xtt)))]
+    bases = [
+        pltpu.make_async_copy(tables.at[AT_Y], tab_y, table.at[0]),
+        pltpu.make_async_copy(tables.at[AT_X], tab.at[pl.ds(0, 8)], table.at[1]),
+        pltpu.make_async_copy(tables.at[AT_XT], tab.at[pl.ds(8, 8)], table.at[2]),
+    ]
+    limits = pltpu.make_async_copy(cut_at, cut, scalar)
     loads[0].start()
-    tables[0].start()
+    bases[0].start()
 
     barrier = pltpu.get_barrier_semaphore()
 
@@ -93,7 +111,7 @@
     lax.fori_loop(1, SLABS, greet, 0)
     for e in (after, before):
         pl.semaphore_signal(barrier, 1, device_id={"ens": e, "slab": me}, device_id_type=MESH)
-    for copy in (loads[1], loads[2], tables[1], tables[2]):
+    for copy in (loads[1], loads[2], bases[1], bases[2], limits):
         copy.start()
 
     def spread(source, target, c, sent, landed):
@@ -111,15 +129,31 @@
         blocks = buffer.at[c, pl.ds(0, SLABS - 1)]
         pltpu.make_async_copy(blocks, blocks, sem.at[c]).wait()
 
+    def half_of(buffer, h, sem):
+        blocks = buffer.at[pl.ds(0, SLABS - 1)]
+        pltpu.make_async_copy(blocks, blocks, sem.at[2 + h]).wait()
+
+    def spread_half(source, target, h, sent, landed):
+        def one(i, _):
+            t = other(i)
+            pltpu.make_async_remote_copy(
+                source.at[2, t, :, pl.ds(128 * h, 128)], target.at[me], sent.at[2 + h], landed.at[2 + h],
+                device_id={"ens": ens, "slab": t}, device_id_type=MESH,
+            ).start()
+            return 0
+
+        lax.fori_loop(1, SLABS, one, 0)
+
     def analyse(c):
         pltpu.make_async_copy(vel.at[c], u.at[c], load.at[c]).wait()
         left, right = u[c, :, :512], u[c, :, 512:]
         for parity in (0, 1):
             high, low = split(left + right if parity == 0 else left - right)
-            total = dot_nt(yt[parity, 0], high) + (dot_nt(yt[parity, 0], low) + dot_nt(yt[parity, 1], high))
+            y_high, y_low = tab_y[parity, :256], tab_y[parity, 256:]
+            total = dot_nt(y_high, high) + (dot_nt(y_high, low) + dot_nt(y_low, high))
             spec[c, pl.ds(32 * parity, 32)] = total.reshape(32, 8, 256)
 
-    tables[0].wait()
+    bases[0].wait()
     analyse(0)
     pl.semaphore_wait(barrier, SLABS + 1)
 
@@ -134,6 +168,7 @@
 
     lax.fori_loop(0, 3, forward, 0)
 
+    limits.wait()
     row = lax.broadcasted_iota(jnp.int32, (8, 512), 0)
     column = lax.broadcasted_iota(jnp.int32, (8, 512), 1)
     ky = 2 * ((8 * me + row) % 128) + lax.div(me, 32)
@@ -142,15 +177,15 @@
         kx = 2 * (column % 256) + parity
         weight = weight_y * (jnp.where(kx == 0, 1.0, 2.0) / 2048.0)
         for z in range(8):
-            kept = jnp.logical_and(kx <= cut[0, z], ky <= cut[1, z])
+            kept = jnp.logical_and(kx <= cut[0, 0, z], ky <= cut[0, 1, z])
             mask[parity, pl.ds(8 * z, 8), :] = jnp.where(kept, weight, 0.0)
     lane = lax.broadcasted_iota(jnp.int32, (8, 128), 1)
     for q in range(16):
         offset = jnp.abs(128 * q + lane - bound[0])
         distance = jnp.minimum(offset, 2048 - offset)
         relax[q] = jnp.exp(-distance.astype(F32) / 512.0)
-    tables[1].wait()
-    tables[2].wait()
+    bases[1].wait()
+    bases[2].wait()
 
     def filter_chunk(c, _):
         all_of(recv, c, recv_f)
@@ -168,13 +203,16 @@
 
         lax.fori_loop(0, 8, gather, 0)
         for parity in (0, 1):
-            both = dot(data[parity], xt[parity, 0])
-            kept = (both[:64] + (both[64:] + dot(data[parity, :64], xt[parity, 1]))) * mask[parity]
+            x_high, x_low = (tab[pl.ds(4 * parity + 2 * i, 2)].reshape(1024, 512) for i in (0, 1))
+            both = dot(data[parity], x_high)
+            kept = (both[:64] + (both[64:] + dot(data[parity, :64], x_low))) * mask[parity]
             high, low = split(kept)
             coef[:64] = high
             coef[64:] = low
-            both = dot(coef[...], xtt[parity, 0])
-            parts[parity] = both[:64] + (both[64:] + dot(coef[:64], xtt[parity, 1]))
+            for side in (0, 1):
+                both = dot(coef[...], tab[8 + 4 * parity + side])
+                low = dot(coef[:64], tab[10 + 4 * parity + side])
+                parts[parity, :, pl.ds(512 * side, 512)] = both[:64] + (both[64:] + low)
 
         xi = lax.broadcasted_iota(jnp.int32, (64, 128), 1)
 
@@ -210,75 +248,112 @@
             return 0
 
         lax.fori_loop(0, 8, scatter, 0)
-        spread(back, ret, c, send_r, recv_r)
-        ret[c, me] = back[c, me]
+
+        @pl.when(c < 2)
+        def _():
+            spread(back, ret, c, send_r, recv_r)
+            ret[c, me] = back[c, me]
+
+        @pl.when(c == 2)
+        def _():
+            for h, target in enumerate((ret_half, last_out)):
+                spread_half(back, target, h, send_r, recv_r)
+                target[me] = back[2, me, :, pl.ds(128 * h, 128)]
+
         return 0
 
     lax.fori_loop(0, 3, filter_chunk, 0)
 
+    def early(c, _):
+        all_of(ret, c, recv_r)
+        synthesise(ret[c].reshape(512, 256), tab_y, first_out.at[c])
+        return 0
+
+    lax.fori_loop(0, 2, early, 0)
+    half_of(ret_half, 0, recv_r)
+    synthesise(ret_half[...].reshape(512, 128), tab_y, second_out)
+
     def finish(c, _):
-        all_of(recv, c, send_f)
-        all_of(recv, c, send_r)
-        all_of(recv, c, recv_r)
+        all_of(spec, c, send_f)
         pltpu.make_async_copy(plane_out.at[c], plane_out.at[c], send_p.at[c]).wait()
         return 0
 
     lax.fori_loop(0, 3, finish, 0)
-
-
-def synthesis_kernel(ret, yt, out):
-    halves = []
-    for parity in (0, 1):
-        high, low = split(ret[0, pl.ds(256 * parity, 256), :].T)
-        halves.append(dot(high, yt[parity, 0]) + (dot(low, yt[parity, 0]) + dot(high, yt[parity, 1])))
-    out[0, :, :512] = halves[0] + halves[1]
-    out[0, :, 512:] = halves[0] - halves[1]
+    for c in (0, 1):
+        all_of(back, c, send_r)
+    for h in (0, 1):
+        half_of(ret_half, h, send_r)
+    half_of(last_out, 1, recv_r)
+
+
+def emit_kernel(first, second, last, tab_y, out, rest, sem):
+    copies = [
+        pltpu.make_async_copy(first, out.at[pl.ds(0, 2)], sem.at[0]),
+        pltpu.make_async_copy(second, out.at[2, pl.ds(0, 128)], sem.at[1]),
+        pltpu.make_async_copy(rest, out.at[2, pl.ds(128, 128)], sem.at[2]),
+    ]
+    copies[0].start()
+    copies[1].start()
+    synthesise(last[...].reshape(512, 128), tab_y, rest)
+    copies[2].start()
+    for copy in copies:
+        copy.wait()
+
+
+def in_hbm(array):
+    return pltpu.with_memory_space_constraint(array, pltpu.HBM)
 
 
 def on_device(velocity, cutoffs, plane_index, boundary_index):
-    ytab = jnp.asarray(np.ascontiguousarray(half_basis(1024, KY).transpose(0, 1, 3, 2)))
+    y_basis = half_basis(1024, KY).transpose(0, 1, 3, 2).reshape(2, 512, 512)
     x_basis = half_basis(2048, KX)
-    xtab = jnp.asarray(x_basis)
-    xtab_t = jnp.asarray(np.ascontiguousarray(x_basis.transpose(0, 1, 3, 2)))
-    anywhere = pl.BlockSpec(memory_space=pltpu.HBM)
-    smem = pl.BlockSpec(memory_space=pltpu.SMEM)
+    x_back = x_basis.transpose(0, 1, 3, 2).reshape(2, 2, 512, 2, 512).transpose(0, 1, 3, 2, 4).reshape(8, 512, 512)
+    tables = jnp.asarray(np.concatenate([y_basis, x_basis.reshape(8, 512, 512), x_back]))
+    smem, vmem = pltpu.SMEM, pltpu.VMEM
+    here = pl.BlockSpec(memory_space=vmem)
+    anywhere = pl.BlockSpec(memory_space=pl.ANY)
     dma = pltpu.SemaphoreType.DMA
-    blocks = pltpu.VMEM((3, SLABS, 8, 256), F32)
-    ret = pl.pallas_call(
+    blocks = vmem((3, SLABS, 8, 256), F32)
+    scalar = pl.BlockSpec(memory_space=smem)
+    pieces = pl.pallas_call(
         filter_kernel,
-        out_shape=jax.ShapeDtypeStruct((3, SLABS, 8, 256), F32),
-        in_specs=[anywhere, smem, smem, smem, anywhere, anywhere, anywhere],
-        out_specs=pl.BlockSpec(memory_space=pltpu.VMEM),
+        out_shape=[
+            jax.ShapeDtypeStruct((2, 256, 1024), F32),
+            jax.ShapeDtypeStruct((128, 1024), F32),
+            jax.ShapeDtypeStruct((SLABS, 8, 128), F32),
+            jax.ShapeDtypeStruct((2, 512, 512), BF16),
+        ],
+        in_specs=[anywhere, anywhere, scalar, scalar, anywhere],
+        out_specs=[here] * 4,
         scratch_shapes=[
-            pltpu.VMEM((3, 256, 1024), F32),
-            pltpu.VMEM(ytab.shape, BF16),
-            pltpu.VMEM(xtab.shape, BF16),
-            pltpu.VMEM(xtab_t.shape, BF16),
+            smem((1, 2, 8), jnp.int32),
+            vmem((3, 256, 1024), F32),
+            vmem((16, 512, 512), BF16),
             blocks,
             blocks,
-            pltpu.VMEM((2, 128, 1024), BF16),
-            pltpu.VMEM((2, 64, 512), F32),
-            pltpu.VMEM((128, 512), BF16),
-            pltpu.VMEM((2, 64, 1024), F32),
-            pltpu.VMEM((2, 64, 1024), F32),
+            vmem((2, 128, 1024), BF16),
+            vmem((2, 64, 512), F32),
+            vmem((128, 512), BF16),
+            vmem((2, 64, 1024), F32),
+            vmem((2, 64, 1024), F32),
             blocks,
-            pltpu.VMEM((16, 8, 128), F32),
-            pltpu.VMEM((3, 64, 128), F32),
-            pltpu.VMEM((3, 64, 128), F32),
+            vmem((2, SLABS, 8, 256), F32),
+            vmem((SLABS, 8, 128), F32),
+            vmem((16, 8, 128), F32),
+            vmem((3, 64, 128), F32),
+            vmem((3, 64, 128), F32),
         ]
-        + [dma((3,))] * 8,
-        compiler_params=pltpu.CompilerParams(collective_id=0, has_side_effects=True, vmem_limit_bytes=48 << 20),
-    )(velocity.reshape(3, 256, 1024), cutoffs[0], plane_index, boundary_index, ytab, xtab, xtab_t)
+        + [dma] + [dma((n,)) for n in (3, 3, 3, 3, 4, 4, 3, 3)],
+        compiler_params=pltpu.CompilerParams(collective_id=0, has_side_effects=True, vmem_limit_bytes=VMEM_GRANT),
+    )(in_hbm(velocity.reshape(3, 256, 1024)), in_hbm(cutoffs), plane_index, boundary_index, in_hbm(tables))
     out = pl.pallas_call(
-        synthesis_kernel,
-        grid=(3,),
+        emit_kernel,
         out_shape=jax.ShapeDtypeStruct((3, 256, 1024), F32),
-        in_specs=[
-            pl.BlockSpec((1, 512, 256), lambda i: (i, 0, 0)),
-            pl.BlockSpec(ytab.shape, lambda i: (0, 0, 0, 0)),
-        ],
-        out_specs=pl.BlockSpec((1, 256, 1024), lambda i: (i, 0, 0)),
-    )(ret.reshape(3, 512, 256), ytab)
+        in_specs=[here] * 4,
+        out_specs=anywhere,
+        scratch_shapes=[vmem((128, 1024), F32), dma((3,))],
+        compiler_params=pltpu.CompilerParams(vmem_limit_bytes=16 << 20),
+    )(*pieces)
     return out.reshape(velocity.shape)
 
 

time: 94.6 us -> 85.4 us (0.903)
  local copies, waits for them, and re-layouts: 4.95 us -> 0 us
  Pallas kernels: 88.1 us -> 84 us
    unnamed x8 -> x0, local copies, waits for them, and re-layouts: 4.95 us -> none
    pallas_call x2, Pallas kernels: 88.1 us -> 84 us  [the longest x1 82.3 us: on_device(): pl.pallas_call(filter_kernel, out_shape=[jax.ShapeDtypeStruct((2, 256, 10...]
where the time goes in v1:
time: 85.4 us; the launch traced here: 85.3 us
  Pallas kernels  84 us (98%)
  between operations  1.3 us (2%)
    pallas_call x1, Pallas kernels, on_device(): pl.pallas_call(filter_kernel, out_shape=[jax.ShapeDtypeStruct((2, 256, 10...  82.3 us

profile of v1, /device:TPU:1, one launch (start us, length us, event | category | flops | bytes accessed | tf_op | source)
XLA Modules:
  0.0 85.3 jit_solution(11209087514307824937)
XLA Ops:
  1.3 82.3 %shard_map.55 = (f32[2,256,1024]{2,1,0:T(8,128)S(1)}, f32[128,1024]{1,0:T(8,128)S(1)}, f32[64,8,128]{2,1,0:T(8,128)S(1)}, bf16[2,512,512]{2,1,0:T(8,128)(2,1)S(1)}) custom-call(f32[3,256,1024]{2,1,0:T(8,128)} %bitcast.2, s32[1,2,8]{2,1,0:T(2,128)} %cut_at.1, s32[1]{0:T(128)S(6)} %copy.6.plane, s32[1]{0:T(128)S(6)} %copy.7.bound, ...), custom_call_target="tpu_custom_call" | custom-call | tf_op jit(solution)/shard_map/pallas_call | solution.py:318
  83.6 1.7 %shard_map.56 = f32[3,256,1024]{2,1,0:T(8,128)} custom-call(f32[2,256,1024]{2,1,0:T(8,128)S(1)} %get-tuple-element.9.first, f32[128,1024]{1,0:T(8,128)S(1)} %get-tuple-element.10.second, f32[64,8,128]{2,1,0:T(8,128)S(1)} %get-tuple-element.11.last, bf16[2,512,512]{2,1,0:T(8,128)(2,1)S(1)} %get-tuple-element.12.tab_y), custom_call_target="tpu_custom_call" | custom-call | tf_op jit(solution)/shard_map/pallas_call | solution.py:349

commit v2 on v1

--- a/solution.py
+++ b/solution.py
@@ -92,6 +92,11 @@
         dy, dc = 3 - lax.rem(lax.div(i, 2), 4), 1 - lax.rem(i, 2)
         return lax.rem(my_y + dy, 4) * 16 + lax.rem(my_z + dz, 8) * 2 + lax.rem(my_c + dc, 2)
 
+    def served(i):
+        step = lax.div(i, 8)
+        z = step + lax.div(step, 5) * (12 - 2 * step)
+        return lax.rem(my_y + lax.rem(lax.div(i, 2), 4), 4) * 16 + z * 2 + lax.rem(my_c + lax.rem(i, 2), 2)
+
     loads = [pltpu.make_async_copy(vel.at[c], u.at[c], load.at[c]) for c in range(3)]
     bases = [
         pltpu.make_async_copy(tables.at[AT_Y], tab_y, table.at[0]),
@@ -133,16 +138,19 @@
         blocks = buffer.at[pl.ds(0, SLABS - 1)]
         pltpu.make_async_copy(blocks, blocks, sem.at[2 + h]).wait()
 
-    def spread_half(source, target, h, sent, landed):
+    def give_back(source, target, sent, landed):
         def one(i, _):
-            t = other(i)
-            pltpu.make_async_remote_copy(
-                source.at[2, t, :, pl.ds(128 * h, 128)], target.at[me], sent.at[2 + h], landed.at[2 + h],
-                device_id={"ens": ens, "slab": t}, device_id_type=MESH,
-            ).start()
+            t = served(i)
+
+            @pl.when(t != me)
+            def _():
+                pltpu.make_async_remote_copy(
+                    source(t), target.at[me], sent, landed, device_id={"ens": ens, "slab": t}, device_id_type=MESH
+                ).start()
+
             return 0
 
-        lax.fori_loop(1, SLABS, one, 0)
+        lax.fori_loop(0, SLABS, one, 0)
 
     def analyse(c):
         pltpu.make_async_copy(vel.at[c], u.at[c], load.at[c]).wait()
@@ -251,13 +259,13 @@
 
         @pl.when(c < 2)
         def _():
-            spread(back, ret, c, send_r, recv_r)
+            give_back(lambda t: back.at[c, t], ret.at[c], send_r.at[c], recv_r.at[c])
             ret[c, me] = back[c, me]
 
         @pl.when(c == 2)
         def _():
             for h, target in enumerate((ret_half, last_out)):
-                spread_half(back, target, h, send_r, recv_r)
+                give_back(lambda t: back.at[2, t, :, pl.ds(128 * h, 128)], target, send_r.at[2 + h], recv_r.at[2 + h])
                 target[me] = back[2, me, :, pl.ds(128 * h, 128)]
 
         return 0

time: 85.4 us -> 84 us (0.984)
  Pallas kernels: 84 us -> 82.6 us
    pallas_call x1, Pallas kernels: 82.3 us -> 80.9 us  [on_device(): pl.pallas_call(filter_kernel, out_shape=[jax.ShapeDtypeStruct((2, 256, 10...]
where the time goes in v2:
time: 84 us; the launch traced here: 83.9 us
  Pallas kernels  82.6 us (98%)
  between operations  1.3 us (2%)
    pallas_call x1, Pallas kernels, on_device(): pl.pallas_call(filter_kernel, out_shape=[jax.ShapeDtypeStruct((2, 256, 10...  80.9 us
    pallas_call x1, Pallas kernels, on_device(): pl.pallas_call(emit_kernel, out_shape=jax.ShapeDtypeStruct((3, 256, 1024)...  1.68 us

profile of v2, /device:TPU:1, one launch (start us, length us, event | category | flops | bytes accessed | tf_op | source)
XLA Modules:
  0.0 83.9 jit_solution(15986629185438573651)
XLA Ops:
  1.3 80.9 %shard_map.55 = (f32[2,256,1024]{2,1,0:T(8,128)S(1)}, f32[128,1024]{1,0:T(8,128)S(1)}, f32[64,8,128]{2,1,0:T(8,128)S(1)}, bf16[2,512,512]{2,1,0:T(8,128)(2,1)S(1)}) custom-call(f32[3,256,1024]{2,1,0:T(8,128)} %bitcast.2, s32[1,2,8]{2,1,0:T(2,128)} %cut_at.1, s32[1]{0:T(128)S(6)} %copy.6.plane, s32[1]{0:T(128)S(6)} %copy.7.bound, ...), custom_call_target="tpu_custom_call" | custom-call | tf_op jit(solution)/shard_map/pallas_call | solution.py:326
  82.3 1.7 %shard_map.56 = f32[3,256,1024]{2,1,0:T(8,128)} custom-call(f32[2,256,1024]{2,1,0:T(8,128)S(1)} %get-tuple-element.9.first, f32[128,1024]{1,0:T(8,128)S(1)} %get-tuple-element.10.second, f32[64,8,128]{2,1,0:T(8,128)S(1)} %get-tuple-element.11.last, bf16[2,512,512]{2,1,0:T(8,128)(2,1)S(1)} %get-tuple-element.12.tab_y), custom_call_target="tpu_custom_call" | custom-call | tf_op jit(solution)/shard_map/pallas_call | solution.py:357

commit v3 on v2

--- a/solution.py
+++ b/solution.py
@@ -13,6 +13,7 @@
 KX = 512
 KY = 256
 SLABS = 64
+FAR = 25
 VMEM_GRANT = 36 << 20
 AT_Y, AT_X, AT_XT = pl.ds(0, 2), pl.ds(2, 8), pl.ds(10, 8)
 F32 = jnp.float32
@@ -78,7 +79,7 @@
     vel, cut_at, plane, bound, tables,
     first_out, second_out, last_out, tab_y,
     cut, u, tab, spec, recv, data, mask, coef, parts, field, back, ret, ret_half, relax, plane_out, plane_in,
-    scalar, load, table, send_f, recv_f, send_r, recv_r, send_p, recv_p,
+    scalar, load, table, send_f, recv_f, send_r, recv_r, send_p, recv_p, ready,
 ):
     ens = lax.axis_index("ens")
     me = lax.axis_index("slab")
@@ -113,13 +114,13 @@
         pl.semaphore_signal(barrier, 1, device_id={"ens": ens, "slab": other(i)}, device_id_type=MESH)
         return 0
 
-    lax.fori_loop(1, SLABS, greet, 0)
+    lax.fori_loop(FAR, SLABS, greet, 0)
     for e in (after, before):
         pl.semaphore_signal(barrier, 1, device_id={"ens": e, "slab": me}, device_id_type=MESH)
     for copy in (loads[1], loads[2], bases[1], bases[2], limits):
         copy.start()
 
-    def spread(source, target, c, sent, landed):
+    def spread(source, target, c, sent, landed, first=1, end=SLABS):
         def one(i, _):
             t = other(i)
             pltpu.make_async_remote_copy(
@@ -128,7 +129,7 @@
             ).start()
             return 0
 
-        lax.fori_loop(1, SLABS, one, 0)
+        lax.fori_loop(first, end, one, 0)
 
     def all_of(buffer, c, sem):
         blocks = buffer.at[c, pl.ds(0, SLABS - 1)]
@@ -163,18 +164,22 @@
 
     bases[0].wait()
     analyse(0)
-    pl.semaphore_wait(barrier, SLABS + 1)
+    pl.semaphore_wait(barrier, SLABS - FAR + 2)
+    for dz in (2, 6):
+        there = my_y * 16 + lax.rem(my_z + dz, 8) * 2 + my_c
+        pl.semaphore_signal(ready, 1, device_id={"ens": ens, "slab": there}, device_id_type=MESH)
+    spread(spec, recv, 0, send_f, recv_f, FAR, SLABS)
+    pl.semaphore_wait(ready, 2)
+    spread(spec, recv, 0, send_f, recv_f, 1, FAR)
+    recv[0, me] = spec[0, me]
 
     def forward(c, _):
-        @pl.when(c > 0)
-        def _():
-            analyse(c)
-
+        analyse(c)
         spread(spec, recv, c, send_f, recv_f)
         recv[c, me] = spec[c, me]
         return 0
 
-    lax.fori_loop(0, 3, forward, 0)
+    lax.fori_loop(1, 3, forward, 0)
 
     limits.wait()
     row = lax.broadcasted_iota(jnp.int32, (8, 512), 0)
@@ -351,7 +356,7 @@
             vmem((3, 64, 128), F32),
             vmem((3, 64, 128), F32),
         ]
-        + [dma] + [dma((n,)) for n in (3, 3, 3, 3, 4, 4, 3, 3)],
+        + [dma] + [dma((n,)) for n in (3, 3, 3, 3, 4, 4, 3, 3)] + [pltpu.SemaphoreType.REGULAR],
         compiler_params=pltpu.CompilerParams(collective_id=0, has_side_effects=True, vmem_limit_bytes=VMEM_GRANT),
     )(in_hbm(velocity.reshape(3, 256, 1024)), in_hbm(cutoffs), plane_index, boundary_index, in_hbm(tables))
     out = pl.pallas_call(

time: 84 us -> 83.2 us (level)
    pallas_call x1, Pallas kernels: 80.9 us -> 80.1 us  [on_device(): pl.pallas_call(filter_kernel, out_shape=[jax.ShapeDtypeStruct((2, 256, 10...]
where the time goes in v3:
time: 83.2 us; the launch traced here: 83.1 us
  Pallas kernels  81.8 us (98%)
  between operations  1.3 us (2%)
    pallas_call x1, Pallas kernels, on_device(): pl.pallas_call(filter_kernel, out_shape=[jax.ShapeDtypeStruct((2, 256, 10...  80.1 us
    pallas_call x1, Pallas kernels, on_device(): pl.pallas_call(emit_kernel, out_shape=jax.ShapeDtypeStruct((3, 256, 1024)...  1.68 us

profile of v3, /device:TPU:1, one launch (start us, length us, event | category | flops | bytes accessed | tf_op | source)
XLA Modules:
  0.0 83.1 jit_solution(10740481799560287443)
XLA Ops:
  1.3 80.1 %shard_map.55 = (f32[2,256,1024]{2,1,0:T(8,128)S(1)}, f32[128,1024]{1,0:T(8,128)S(1)}, f32[64,8,128]{2,1,0:T(8,128)S(1)}, bf16[2,512,512]{2,1,0:T(8,128)(2,1)S(1)}) custom-call(f32[3,256,1024]{2,1,0:T(8,128)} %bitcast.2, s32[1,2,8]{2,1,0:T(2,128)} %cut_at.1, s32[1]{0:T(128)S(6)} %copy.6.plane, s32[1]{0:T(128)S(6)} %copy.7.bound, ...), custom_call_target="tpu_custom_call" | custom-call | tf_op jit(solution)/shard_map/pallas_call | solution.py:331
  81.4 1.7 %shard_map.56 = f32[3,256,1024]{2,1,0:T(8,128)} custom-call(f32[2,256,1024]{2,1,0:T(8,128)S(1)} %get-tuple-element.9.first, f32[128,1024]{1,0:T(8,128)S(1)} %get-tuple-element.10.second, f32[64,8,128]{2,1,0:T(8,128)S(1)} %get-tuple-element.11.last, bf16[2,512,512]{2,1,0:T(8,128)(2,1)S(1)} %get-tuple-element.12.tab_y), custom_call_target="tpu_custom_call" | custom-call | tf_op jit(solution)/shard_map/pallas_call | solution.py:362

commit v4 on v3

--- a/solution.py
+++ b/solution.py
@@ -96,7 +96,7 @@
     def served(i):
         step = lax.div(i, 8)
         z = step + lax.div(step, 5) * (12 - 2 * step)
-        return lax.rem(my_y + lax.rem(lax.div(i, 2), 4), 4) * 16 + z * 2 + lax.rem(my_c + lax.rem(i, 2), 2)
+        return lax.rem(lax.div(i, 2), 4) * 16 + z * 2 + lax.rem(my_c + lax.rem(i, 2), 2)
 
     loads = [pltpu.make_async_copy(vel.at[c], u.at[c], load.at[c]) for c in range(3)]
     bases = [

time: 83.2 us -> 82.6 us (level)
  no operation moved by 1% of the time
where the time goes in v4:
time: 82.6 us; the launch traced here: 82.4 us
  Pallas kernels  81.1 us (98%)
  between operations  1.3 us (2%)
    pallas_call x1, Pallas kernels, on_device(): pl.pallas_call(filter_kernel, out_shape=[jax.ShapeDtypeStruct((2, 256, 10...  79.4 us
    pallas_call x1, Pallas kernels, on_device(): pl.pallas_call(emit_kernel, out_shape=jax.ShapeDtypeStruct((3, 256, 1024)...  1.68 us

profile of v4, /device:TPU:1, one launch (start us, length us, event | category | flops | bytes accessed | tf_op | source)
XLA Modules:
  0.0 82.4 jit_solution(3915439859360688763)
XLA Ops:
  1.3 79.4 %shard_map.55 = (f32[2,256,1024]{2,1,0:T(8,128)S(1)}, f32[128,1024]{1,0:T(8,128)S(1)}, f32[64,8,128]{2,1,0:T(8,128)S(1)}, bf16[2,512,512]{2,1,0:T(8,128)(2,1)S(1)}) custom-call(f32[3,256,1024]{2,1,0:T(8,128)} %bitcast.2, s32[1,2,8]{2,1,0:T(2,128)} %cut_at.1, s32[1]{0:T(128)S(6)} %copy.6.plane, s32[1]{0:T(128)S(6)} %copy.7.bound, ...), custom_call_target="tpu_custom_call" | custom-call | tf_op jit(solution)/shard_map/pallas_call | solution.py:331
  80.7 1.7 %shard_map.56 = f32[3,256,1024]{2,1,0:T(8,128)} custom-call(f32[2,256,1024]{2,1,0:T(8,128)S(1)} %get-tuple-element.9.first, f32[128,1024]{1,0:T(8,128)S(1)} %get-tuple-element.10.second, f32[64,8,128]{2,1,0:T(8,128)S(1)} %get-tuple-element.11.last, bf16[2,512,512]{2,1,0:T(8,128)(2,1)S(1)} %get-tuple-element.12.tab_y), custom_call_target="tpu_custom_call" | custom-call | tf_op jit(solution)/shard_map/pallas_call | solution.py:362

commit v5 on v4

--- a/solution.py
+++ b/solution.py
@@ -95,7 +95,8 @@
 
     def served(i):
         step = lax.div(i, 8)
-        z = step + lax.div(step, 5) * (12 - 2 * step)
+        later = lax.div(step, 4)
+        z = (1 - later) * lax.rem(6 - step, 4) + later * (11 - step)
         return lax.rem(lax.div(i, 2), 4) * 16 + z * 2 + lax.rem(my_c + lax.rem(i, 2), 2)
 
     loads = [pltpu.make_async_copy(vel.at[c], u.at[c], load.at[c]) for c in range(3)]

time: 82.6 us -> 84.5 us (1.023)
  Pallas kernels: 81.1 us -> 83.1 us
    pallas_call x1, Pallas kernels: 79.4 us -> 81.4 us  [on_device(): pl.pallas_call(filter_kernel, out_shape=[jax.ShapeDtypeStruct((2, 256, 10...]
where the time goes in v5:
time: 84.5 us; the launch traced here: 84.4 us
  Pallas kernels  83.1 us (98%)
  between operations  1.3 us (2%)
    pallas_call x1, Pallas kernels, on_device(): pl.pallas_call(filter_kernel, out_shape=[jax.ShapeDtypeStruct((2, 256, 10...  81.4 us

profile of v5, /device:TPU:1, one launch (start us, length us, event | category | flops | bytes accessed | tf_op | source)
XLA Modules:
  0.0 84.4 jit_solution(1608440657739018706)
XLA Ops:
  1.3 81.4 %shard_map.55 = (f32[2,256,1024]{2,1,0:T(8,128)S(1)}, f32[128,1024]{1,0:T(8,128)S(1)}, f32[64,8,128]{2,1,0:T(8,128)S(1)}, bf16[2,512,512]{2,1,0:T(8,128)(2,1)S(1)}) custom-call(f32[3,256,1024]{2,1,0:T(8,128)} %bitcast.2, s32[1,2,8]{2,1,0:T(2,128)} %cut_at.1, s32[1]{0:T(128)S(6)} %copy.6.plane, s32[1]{0:T(128)S(6)} %copy.7.bound, ...), custom_call_target="tpu_custom_call" | custom-call | tf_op jit(solution)/shard_map/pallas_call | solution.py:332
  82.7 1.7 %shard_map.56 = f32[3,256,1024]{2,1,0:T(8,128)} custom-call(f32[2,256,1024]{2,1,0:T(8,128)S(1)} %get-tuple-element.9.first, f32[128,1024]{1,0:T(8,128)S(1)} %get-tuple-element.10.second, f32[64,8,128]{2,1,0:T(8,128)S(1)} %get-tuple-element.11.last, bf16[2,512,512]{2,1,0:T(8,128)(2,1)S(1)} %get-tuple-element.12.tab_y), custom_call_target="tpu_custom_call" | custom-call | tf_op jit(solution)/shard_map/pallas_call | solution.py:363
